TPU v7x, 256 devices: a 8x8x2 block of a 8x8x16 slice. The times are simulated.
256 devices in a mesh: grp: 2 (over z), kv: 128 (over y, x, core).
Axes of the slice: x: 8, y: 8, z: 2, core: 2. Of those that a mesh axis runs over, the one named last changes fastest.
The devices are a block of a 8x8x16 slice.
Arguments:
- queries: bfloat16 [1024, 40, 128], P(('grp', 'kv')), parts along dimension 0, may hold values from -250 to 250
- cache_keys: bfloat16 [65536, 40, 128], P(('grp', 'kv')), parts along dimension 0, may hold values from -8 to 8
- cache_values: bfloat16 [65536, 40, 128], P(('grp', 'kv')), parts along dimension 0, may hold values from -18 to 18
- new_keys: bfloat16 [1024, 40, 128], P(('grp', 'kv')), parts along dimension 0, may hold values from -4 to 4
- new_values: bfloat16 [1024, 40, 128], P(('grp', 'kv')), parts along dimension 0, may hold values from -4 to 4
- valid_frames: int32 [2], P('grp'), parts along dimension 0, may hold values from 64 to 128
Outputs:
- attended: bfloat16 [1024, 40, 128], P(('grp', 'kv')), parts along dimension 0
There are 2 independent parts, one for each index of `grp`. A program takes and returns all parts, laid end to end along the dimension named above; each array names one. Nothing has to cross between parts.
All inputs are finite; a program needn't handle non-finite values.
Results may differ from a plain program's by a relative error of at most 0.0027.
Values may be sent and summed in bfloat16 or wider, within the bound.
A program may use at most 128 MiB of HBM per device.

v0:
```python
import functools
import math

import jax
import jax.numpy as jnp
from jax import lax
from jax.experimental import pallas as pl
from jax.experimental.pallas import tpu as pltpu
from jax.sharding import Mesh
from jax.sharding import PartitionSpec as P

FRAME = 256
RING = (8, 8, 2)
GRP_KV = ("grp", "kv_0", "kv_1", "kv_2")
GROUPS = 5
RC = 32
PC = 512
NEG = -1e30
ROUTES = ((4, 2), (3, 1), (1, 1), (-3, -1), (-1, -1), (2, 2), (-2, -2))
BATCHES = ((0, 2), (2, 4), (4, 5))
LOG2E = math.log2(math.e)
TOP = 32767.0
MESH = pl.DeviceIdType.MESH
NT = (((1,), (1,)), ((), ()))


def steps_of(n, way):
    return n // 2 if way == 0 else n - 1 - n // 2


def plan():
    ny, nx, _ = RING
    ids, outs = {}, {}
    for name in ("q", "n", "k", "v", "fin"):
        ids[name] = len(ids)
        outs[name] = len(outs)
    for s in range(2):
        for m in range(nx):
            ids["p1", s, m] = len(ids)
        for e in range(nx // 2):
            for way in range(2):
                for k in range(steps_of(ny, way)):
                    ids["p2", s, e, way, k] = len(ids)
        for g in range(GROUPS):
            for t in range(len(ROUTES)):
                ids["p3", g, s, t] = len(ids)
            outs["p3", g, s] = len(outs)
        for b in range(len(BATCHES)):
            ids["p4", b, s] = len(ids)
            outs["p4", b, s] = len(outs)
        outs["ag", s] = len(outs)
    return ids, outs


def kernel(
    vf, q_hbm, k_hbm, v_hbm, nk_hbm, nv_hbm, out_ref,
    qraw, nraw, kraw, vraw, krel, vrel, kpart, vpart, nrel, qtmp, qbuf,
    score, weight, obuf, raw_stat, stat, rbuf, red, got,
    fin, finrecv, send_sem, recv_sem, local_sem,
):
    ny, nx, _ = RING
    ids, outs = plan()
    y, x, c = lax.axis_index("kv_0"), lax.axis_index("kv_1"), lax.axis_index("kv_2")
    pc = 1 - c
    tok, heads, dim = q_hbm.shape
    cached = k_hbm.shape[0]
    half = heads // 2
    per = half // (2 * GROUPS)
    chip_tok = 2 * tok
    coord = ((y, x), (x, y))
    n = ny
    rows = n * chip_tok
    queries = ny * nx * chip_tok
    c1 = LOG2E / math.sqrt(dim)
    partner = {"kv_2": pc}

    def device(s, major, minor):
        return {"kv_0": major if s == 0 else minor, "kv_1": minor if s == 0 else major}

    def remote(name, src, dst, dev, out=None, at=0):
        return pltpu.make_async_remote_copy(
            src_ref=src, dst_ref=dst,
            send_sem=send_sem.at[outs[name if out is None else out]],
            recv_sem=recv_sem.at[ids[name] + at], device_id=dev, device_id_type=MESH,
        )

    loads = [
        pltpu.make_async_copy(src, dst, local_sem.at[i])
        for i, (src, dst) in enumerate((
            (q_hbm, qraw.at[c]), (nk_hbm, nraw.at[c, 0]), (nv_hbm, nraw.at[c, 1]),
            (k_hbm, kraw), (v_hbm, vraw),
        ))
    ]
    for copy in loads:
        copy.start()
    barrier = pltpu.get_barrier_semaphore()
    peers = [partner]
    peers += [{"kv_0": lax.rem(y + d, ny)} for d in range(1, ny)]
    peers += [{"kv_1": lax.rem(x + d, nx)} for d in range(1, nx)]
    for dev in peers:
        pl.semaphore_signal(barrier, inc=1, device_id=dev, device_id_type=MESH)
    raw_stat[...] = jnp.zeros_like(raw_stat)
    nrel[...] = jnp.zeros_like(nrel)
    for i in range(3):
        loads[i].wait()
    pl.semaphore_wait(barrier, len(peers))

    qswap = remote("q", qraw.at[c], qraw.at[c], partner)
    qswap.start()
    nswap = remote("n", nraw.at[c], nraw.at[c], partner)
    nswap.start()

    def to_heads(value):
        wide = value.astype(jnp.float32)
        return [
            jnp.swapaxes(wide[:, h : h + 8], 0, 1).astype(jnp.bfloat16)
            for h in range(0, heads, 8)
        ]

    qswap.wait_recv()
    for i, part in enumerate(to_heads(qraw[...].reshape(chip_tok, heads, dim))):
        qtmp[8 * i : 8 * i + 8] = part

    for s in range(2):
        major, minor = coord[s]
        qbuf[s, major * n + minor] = qtmp[pl.ds(c * half + s * half // 2, half // 2)]

    def p1_copy(s, to, source):
        major, minor = coord[s]
        ref = qbuf.at[s, major * n + source]
        return remote(("p1", s, 0), ref, ref, device(s, major, to), ("ag", s), source)

    near = sorted(range(n), key=lambda d: min(d, n - d))
    for d in near[1:]:
        for s in range(2):
            minor = coord[s][1]
            p1_copy(s, lax.rem(minor + d, n), minor).start()

    def sign_of(i, way):
        return (1 if way == 0 else -1) * (1 if i % 2 == 0 else -1)

    def pair_at(s, e):
        return 2 * lax.rem(lax.div(coord[s][1], 2) + e, n // 2)

    def p2_copy(s, e, way, k):
        major, minor = coord[s]
        sign = sign_of(e, way)
        ref = qbuf.at[s, pl.ds(lax.rem(major - sign * k + n, n) * n + pair_at(s, e), 2)]
        dev = device(s, lax.rem(major + sign + n, n), minor)
        return remote(("p2", s, e, way, k), ref, ref, dev, ("ag", s))

    def p2_step(k, e):
        for s in range(2):
            minor = coord[s][1]
            if k == 0:
                if e == 0:
                    sibling = minor + 1 - 2 * lax.rem(minor, 2)
                    p1_copy(s, minor, sibling).wait_recv()
                else:
                    for one in range(2):
                        p1_copy(s, minor, pair_at(s, e) + one).wait_recv()
            for way in range(2):
                if 1 <= k <= steps_of(n, way):
                    p2_copy(s, e, way, k - 1).wait_recv()
                if k < steps_of(n, way):
                    p2_copy(s, e, way, k).start()

    gather = [
        functools.partial(p2_step, k, e) for k in range(steps_of(n, 0) + 1)
        for e in (0, 1, n // 2 - 1, 2)
    ]

    CH = 32

    def relayout(raw, rel, i):
        at = i * CH
        for j, piece in enumerate(to_heads(raw[at : at + CH])):
            rel[8 * j : 8 * j + 8, at : at + CH, :] = piece

    kswap = remote("k", krel.at[pl.ds(pc * half, half)], kpart, partner)
    vswap = remote("v", vrel.at[pl.ds(pc * half, half)], vpart, partner)

    def cache_part(raw, rel, load, swap, i):
        if i == 0:
            load.wait()
        relayout(raw, rel, i)
        if i == cached // CH - 1:
            swap.start()

    def news():
        nswap.wait_recv()
        for which in range(2):
            value = jnp.concatenate([nraw[0, which], nraw[1, which]], axis=0)
            for i, part in enumerate(to_heads(value)):
                nrel[which, 8 * i : 8 * i + 8, 0:chip_tok, :] = part

    prepare = [
        functools.partial(cache_part, kraw, krel, loads[3], kswap, i) for i in range(cached // CH)
    ]
    prepare += [
        functools.partial(cache_part, vraw, vrel, loads[4], vswap, i) for i in range(cached // CH)
    ]
    prepare += [news]

    def interleave(first, second, span):
        merged = sorted(
            [((i + 0.5) / len(first) * span, 0, i, f) for i, f in enumerate(first)]
            + [((i + 1.0) / len(second), 1, i, f) for i, f in enumerate(second)],
            key=lambda entry: entry[:3],
        )
        for entry in merged:
            entry[3]()

    interleave(prepare, gather, 0.8)
    kswap.wait_recv()
    vswap.wait_recv()

    index = (y * nx + x) * 2 + c
    live_own = index < vf[0]
    live_par = index + pc - c < vf[0]
    n_heads = half

    def split(i):
        g, r = lax.div(i, 2 * per), lax.rem(i, 2 * per)
        s, j = lax.div(r, per), lax.rem(r, per)
        return g, s, j, (s * GROUPS + g) * per + j

    def scores(i, slot):
        g, s, j, hh = split(i)
        q = qbuf[s, :, g * per + j].reshape(queries, dim)
        for key, lo in ((krel[c * half + hh], 0), (kpart[hh], cached), (nrel[0, c * half + hh], 2 * cached)):
            score[slot, :, lo : lo + key.shape[0]] = lax.dot_general(
                q, key, NT, preferred_element_type=jnp.float32
            )

    lane = lax.broadcasted_iota(jnp.int32, (8, 128), 1)

    def keep(which, i, r0, value):
        g, s, j, _ = split(i)
        for at in range(0, value.shape[0], rows):
            place, first = divmod(r0 + at, rows)
            acc = raw_stat[which, s * GROUPS + g, place]
            for r in range(0, min(rows, value.shape[0]), 8):
                mask = lane == 16 * ((first + r) // 8) + j
                acc = jnp.where(mask, jnp.broadcast_to(value[at + r : at + r + 8], (8, 128)), acc)
            raw_stat[which, s * GROUPS + g, place] = acc

    def softmax(i, slot):
        for r0 in range(0, queries, RC):
            so = score[slot, r0 : r0 + RC, 0:cached]
            sp = score[slot, r0 : r0 + RC, cached : 2 * cached]
            sn = score[slot, r0 : r0 + RC, 2 * cached : 2 * cached + 128]
            lanes = lax.broadcasted_iota(jnp.int32, sn.shape, 1)
            sn = jnp.where(lanes < chip_tok, sn, NEG)

            def fold(op, value):
                return op(value[:, :128], value[:, 128:])

            both = jnp.maximum(
                jnp.where(live_own, fold(jnp.maximum, so), NEG),
                jnp.where(live_par, fold(jnp.maximum, sp), NEG),
            )
            top = jnp.max(jnp.maximum(both, sn), axis=1, keepdims=True)
            po = jnp.exp2((so - jnp.where(live_own, top, -NEG)) * c1)
            pp = jnp.exp2((sp - jnp.where(live_par, top, -NEG)) * c1)
            pn = jnp.exp2((sn - top) * c1)
            total = jnp.sum(
                fold(jnp.add, po) + fold(jnp.add, pp) + pn, axis=1, keepdims=True
            )
            weight[slot, r0 : r0 + RC, 0:cached] = po.astype(jnp.bfloat16)
            weight[slot, r0 : r0 + RC, cached : 2 * cached] = pp.astype(jnp.bfloat16)
            weight[slot, r0 : r0 + RC, 2 * cached :] = pn.astype(jnp.bfloat16)
            keep(0, i, r0, top)
            keep(1, i, r0, total)

    def values(i, slot):
        hh = split(i)[3]
        for r0 in range(0, queries, PC):
            o = None
            for value, lo in ((vrel[c * half + hh], 0), (vpart[hh], cached), (nrel[1, c * half + hh], 2 * cached)):
                term = jnp.dot(
                    weight[slot, r0 : r0 + PC, lo : lo + value.shape[0]], value,
                    preferred_element_type=jnp.float32,
                )
                o = term if o is None else o + term
            big = jnp.maximum(jnp.max(jnp.abs(o), axis=1, keepdims=True), 1e-30)
            o = pack(o * (TOP / big))
            g, s, j, _ = split(i)
            for r in range(0, PC, rows):
                to = pl.ds(pl.multiple_of(j * rows, rows), rows)
                obuf[s * GROUPS + g, (r0 + r) // rows, to, :] = o[r : r + rows]
            keep(2, i, r0, big)

    def pack(value):
        return jnp.round(value).astype(jnp.int32).astype(jnp.int16)

    def unpack(value):
        return value.astype(jnp.int32).astype(jnp.float32)

    place16 = lane % 16
    FINE = 32768.0

    def encode(level, size):
        level_whole, size_whole = jnp.floor(level), jnp.floor(size)
        level_rest = jnp.floor((level - level_whole) * FINE)
        size_rest = jnp.floor((size - size_whole) * FINE)
        low = jnp.where(place16 < 4, level_whole, pltpu.roll(level_rest, 4, 1))
        high = jnp.where(place16 < 12, pltpu.roll(size_whole, 8, 1), pltpu.roll(size_rest, 12, 1))
        return jnp.where(place16 < 8, low, high).astype(jnp.int32).astype(jnp.int16)

    def decode(value):
        level = value + pltpu.roll(value, 124, 1) * (1 / FINE)
        return level, pltpu.roll(level, 120, 1)

    def settle(g):
        for s in range(2):
            gs = s * GROUPS + g
            for place in range(n):
                total = jnp.log(jnp.maximum(raw_stat[1, gs, place], 1e-37)) * LOG2E
                big = jnp.log(jnp.maximum(raw_stat[2, gs, place], 1e-37)) * LOG2E
                level, size = raw_stat[0, gs, place] * c1 + total, big - total
                stat[gs, place, 0] = level
                stat[gs, place, 1] = size
                obuf[gs, place, per * rows :, :] = encode(level, size)

    def combine(pairs):
        top = functools.reduce(jnp.maximum, [level for level, _ in pairs])
        total = functools.reduce(jnp.add, [jnp.exp2(level - top) for level, _ in pairs])
        level = top + jnp.log(total) * LOG2E
        both = [one + size for one, size in pairs]
        most = functools.reduce(jnp.maximum, both)
        parts = [jnp.exp2(one - most) for one in both]
        whole = functools.reduce(jnp.add, parts)
        size = most + jnp.log(whole) * LOG2E - level
        inverse = 1.0 / whole
        return level, size, [part * inverse for part in parts]

    def spread(packed, j, groups):
        one = [
            jnp.broadcast_to(packed[:, 16 * i + j : 16 * i + j + 1], (8, 128)) for i in range(groups)
        ]
        return one[0] if groups == 1 else jnp.concatenate(one, axis=0)

    def slot_of(g, s, t):
        return (2 * g + s) * len(ROUTES) + t

    def along(g, s, steps):
        return lax.rem(coord[s][0] + (steps if g % 2 == 0 else -steps) + n, n)

    def p3_copy(g, s, t, src):
        dev = device(s, along(g, s, ROUTES[t][1]), coord[s][1])
        return remote(("p3", g, s, t), src, rbuf.at[slot_of(g, s, t)], dev, ("p3", g, s))

    per4 = per * chip_tok + 8

    def part_of(g, s, dest):
        gs = s * GROUPS + g
        return obuf.at[gs, dest], (stat[gs, dest, 0], stat[gs, dest, 1])

    def merged(g, s, dest, slots):
        own, own_stat = part_of(g, s, dest)
        pairs = [own_stat] + [decode(unpack(rbuf[at, per * rows :, :])) for at in slots]
        level, size, shares = combine(pairs)
        data = []
        for j in range(per):
            at = pl.ds(j * rows, rows)
            mine = unpack(own[at, :])
            value = mine
            for slot, share in zip(slots, shares[1:]):
                value = value + spread(share, j, n) * (unpack(rbuf[slot, at, :]) - mine)
            data.append(pack(value))
        return data, encode(level, size)

    def p3_step(g, k):
        if k == 0:
            for t in (0, 3, 1, 2, 4):
                for s in range(2):
                    p3_copy(g, s, t, part_of(g, s, along(g, s, ROUTES[t][0]))[0]).start()
            return
        if k == 1:
            for t in (0, 3, 1):
                for s in range(2):
                    p3_copy(g, s, t, rbuf.at[slot_of(g, s, t)]).wait_recv()
            for s in range(2):
                for t, into, sources in ((5, 0, (0, 1)), (6, 3, (3,))):
                    slots = [slot_of(g, s, source) for source in sources]
                    data, code = merged(g, s, along(g, s, ROUTES[t][0]), slots)
                    at = slot_of(g, s, into)
                    for j in range(per):
                        rbuf[at, j * rows : (j + 1) * rows, :] = data[j]
                    rbuf[at, per * rows :, :] = code
            for t, into in ((5, 0), (6, 3)):
                for s in range(2):
                    p3_copy(g, s, t, rbuf.at[slot_of(g, s, into)]).start()
            return
        for t in (2, 4, 5, 6):
            for s in range(2):
                p3_copy(g, s, t, rbuf.at[slot_of(g, s, t)]).wait_recv()
        for s in range(2):
            data, code = merged(g, s, coord[s][0], [slot_of(g, s, t) for t in (2, 4, 5, 6)])
            for m in range(n):
                for j in range(per):
                    at = g * per4 + j * chip_tok
                    red[s, m, at : at + chip_tok, :] = data[j][m * chip_tok : (m + 1) * chip_tok]
                at = g * per4 + per * chip_tok
                red[s, m, at : at + 8, :] = code
        for b, (g0, g1) in enumerate(BATCHES):
            if g == g1 - 1:
                for d in near[:0:-1]:
                    for s in range(2):
                        p4_copy(b, s, d).start()

    def p4_copy(b, s, d):
        major, minor = coord[s]
        to = lax.rem(minor + d, n)
        part = pl.ds(BATCHES[b][0] * per4, (BATCHES[b][1] - BATCHES[b][0]) * per4)
        return remote(
            ("p4", b, s), red.at[s, to, part, :], got.at[s, d - 1, part, :], device(s, major, to)
        )

    def all_of(ref, sem):
        pltpu.make_async_copy(ref, ref, sem).wait()

    def p4_finish(b):
        g0, g1 = BATCHES[b]
        part = pl.ds(g0 * per4, (g1 - g0) * per4)
        for s in range(2):
            all_of(got.at[s, 0 : n - 1, part, :], recv_sem.at[ids["p4", b, s]])
        for s in range(2):
            major, minor = coord[s]
            shift = lax.rem(128 - 16 * minor, 128)
            for g in range(g0, g1):
                first = g * per4
                sources = [red.at[s, minor]] + [got.at[s, d] for d in range(n - 1)]
                pairs = []
                for source in sources:
                    code = unpack(source[first + per * chip_tok : first + per4, :])
                    pairs.append(decode(pltpu.roll(code, shift, 1)))
                top = functools.reduce(jnp.maximum, [level for level, _ in pairs])
                total = functools.reduce(jnp.add, [jnp.exp2(level - top) for level, _ in pairs])
                inverse = 1.0 / (total * TOP)
                parts = [jnp.exp2((level - top) + size) * inverse for level, size in pairs]
                for j in range(per):
                    at = first + j * chip_tok
                    terms = [
                        unpack(source[at : at + chip_tok, :]) * spread(p, j, 1)
                        for source, p in zip(sources, parts)
                    ]
                    fin[(s * GROUPS + g) * per + j] = functools.reduce(jnp.add, terms)

    last = n_heads - 1
    ahead = lambda i: jnp.minimum(i, last)
    scores(0, 0)
    scores(1, 1)
    softmax(0, 0)
    for g in range(GROUPS):
        first = g * 2 * per + 1

        def pair(t, carry):
            i = first + 2 * t
            scores(ahead(i + 1), 0)
            softmax(i, 1)
            values(i - 1, 0)
            scores(ahead(i + 2), 1)
            softmax(ahead(i + 1), 0)
            values(i, 1)
            return carry

        lax.fori_loop(0, per, pair, 0)
        settle(g)
        for gg in range(g, max(g - 3, -1), -1):
            p3_step(gg, g - gg)
    p3_step(GROUPS - 1, 1)
    p3_step(GROUPS - 2, 2)
    p4_finish(0)
    p3_step(GROUPS - 1, 2)
    for b in range(1, len(BATCHES)):
        p4_finish(b)

    tokens = jnp.swapaxes(fin[...], 0, 1)
    qt = jnp.where(c == 0, tokens[:tok], tokens[tok:])
    ot = jnp.where(c == 0, tokens[tok:], tokens[:tok])
    finrecv[0] = ot
    fswap = remote("fin", finrecv.at[0], finrecv.at[1], partner)
    fswap.start()
    fswap.wait_recv()
    theirs = finrecv[1]
    low = jnp.where(c == 0, qt, theirs)
    high = jnp.where(c == 0, theirs, qt)
    out_ref[...] = jnp.concatenate([low, high], axis=1).astype(out_ref.dtype)
    for swap in (qswap, nswap, kswap, vswap, fswap):
        swap.wait_send()
    for s in range(2):
        all_of(qbuf.at[s, 0 : n * n - 1], send_sem.at[outs["ag", s]])
        for g in range(GROUPS):
            all_of(obuf.at[s * GROUPS + g, 0 : n - 1], send_sem.at[outs["p3", g, s]])
        for b, (g0, g1) in enumerate(BATCHES):
            part = pl.ds(g0 * per4, (g1 - g0) * per4)
            all_of(got.at[s, 0 : n - 1, part, :], send_sem.at[outs["p4", b, s]])


def per_device(queries, cache_keys, cache_values, new_keys, new_values, valid_frames):
    ny, nx, _ = RING
    tok, heads, dim = queries.shape
    cached = cache_keys.shape[0]
    assert cached == FRAME and ny == nx == 8
    half = heads // 2
    per = half // (2 * GROUPS)
    chip_tok = 2 * tok
    total = ny * nx * chip_tok
    rows = nx * chip_tok
    ids, outs = plan()
    bf16, i16, f32 = jnp.bfloat16, jnp.int16, jnp.float32
    vmem = pltpu.VMEM
    return pl.pallas_call(
        kernel,
        name="stream_attention",
        out_shape=jax.ShapeDtypeStruct((tok, heads, dim), jnp.bfloat16),
        in_specs=[pl.BlockSpec(memory_space=pltpu.SMEM)]
        + [pl.BlockSpec(memory_space=pl.ANY)] * 5,
        out_specs=pl.BlockSpec(memory_space=pltpu.VMEM),
        scratch_shapes=[
            vmem((2, tok, heads, dim), bf16),
            vmem((2, 2, tok, heads, dim), bf16),
            vmem((cached, heads, dim), bf16),
            vmem((cached, heads, dim), bf16),
            vmem((heads, cached, dim), bf16),
            vmem((heads, cached, dim), bf16),
            vmem((half, cached, dim), bf16),
            vmem((half, cached, dim), bf16),
            vmem((2, heads, 128, dim), bf16),
            vmem((heads, chip_tok, dim), bf16),
            vmem((2, ny * nx, half // 2, chip_tok, dim), bf16),
            vmem((2, total, 2 * cached + 128), f32),
            vmem((2, total, 2 * cached + 128), bf16),
            vmem((2 * GROUPS, ny, per * rows + 8, dim), i16),
            vmem((3, 2 * GROUPS, ny, 8, 128), f32),
            vmem((2 * GROUPS, ny, 2, 8, 128), f32),
            vmem((2 * GROUPS * len(ROUTES), per * rows + 8, dim), i16),
            vmem((2, nx, GROUPS * (per * chip_tok + 8), dim), i16),
            vmem((2, nx - 1, GROUPS * (per * chip_tok + 8), dim), i16),
            vmem((half, chip_tok, dim), f32),
            vmem((2, tok, half, dim), f32),
            pltpu.SemaphoreType.DMA((len(outs),)),
            pltpu.SemaphoreType.DMA((len(ids),)),
            pltpu.SemaphoreType.DMA((5,)),
        ],
        compiler_params=pltpu.CompilerParams(
            collective_id=0, has_side_effects=True, vmem_limit_bytes=60 * 1024 * 1024
        ),
    )(valid_frames, queries, cache_keys, cache_values, new_keys, new_values)


def solution(mesh):
    torus = Mesh(mesh.devices.reshape(mesh.shape["grp"], *RING), GRP_KV)
    return jax.shard_map(
        per_device,
        mesh=torus,
        in_specs=(P(GRP_KV, None, None),) * 5 + (P("grp"),),
        out_specs=P(GRP_KV, None, None),
        check_vma=False,
    )
```

profile of v0, /device:TPU:513, one launch (start us, length us, event | category | flops | bytes accessed | tf_op | source)
XLA Modules:
  0.0 87.9 jit_solution(13711685913617918732)
XLA Ops:
  0.7 85.8 %stream_attention.1 = bf16[4,40,128]{2,1,0:T(8,128)(2,1)} custom-call(s32[1]{0:T(128)S(6)} %copy.8.vf, bf16[4,40,128]{2,1,0:T(8,128)(2,1)} %q_hbm.1, bf16[256,40,128]{2,1,0:T(8,128)(2,1)} %k_hbm.1, bf16[256,40,128]{2,1,0:T(8,128)(2,1)} %v_hbm.1, bf16[4,40,128]{2,1,0:T(8,128)(2,1)} %nk_hbm.1, bf16[4,40,128]{2,1,0:T(8,128)(2,1)} %nv_hbm.1), custom_call_target="tpu_custom_call" | custom-call | tf_op jit(solution)/shard_map/stream_attention/pallas_call | solution.py:515
  86.5 1.4 %copy.9 = bf16[4,40,128]{2,1,0:T(8,128)(2,1)} copy(bf16[4,40,128]{2,1,0:T(8,128)(2,1)} %stream_attention.1) | data formatting | bytes 81920
where the time goes:
time: 88 us; the launch traced here: 87.9 us
  Pallas kernels  85.8 us (98%)
  local copies, waits for them, and re-layouts  1.4 us (2%)
    pallas_call x1, Pallas kernels, per_device(): pl.pallas_call(kernel, name='stream_attention', out_shape=jax.ShapeDtypeS...  85.8 us

commit v1 on v0

--- a/solution.py
+++ b/solution.py
@@ -466,7 +466,8 @@
             values(i, 1)
             return carry
 
-        lax.fori_loop(0, per, pair, 0)
+        for t in range(per):
+            pair(t, 0)
         settle(g)
         for gg in range(g, max(g - 3, -1), -1):
             p3_step(gg, g - gg)

time: 88 us -> 86.7 us (0.985)
  Pallas kernels: 85.8 us -> 84.5 us
    pallas_call x1, Pallas kernels: 85.8 us -> 84.5 us  [per_device(): pl.pallas_call(kernel, name='stream_attention', out_shape=jax.ShapeDtypeS...]
where the time goes in v1:
time: 86.7 us; the launch traced here: 86.6 us
  Pallas kernels  84.5 us (97%)
  local copies, waits for them, and re-layouts  1.4 us (2%)
    pallas_call x1, Pallas kernels, per_device(): pl.pallas_call(kernel, name='stream_attention', out_shape=jax.ShapeDtypeS...  84.5 us

profile of v1, /device:TPU:513, one launch (start us, length us, event | category | flops | bytes accessed | tf_op | source)
XLA Modules:
  0.0 86.6 jit_solution(8625178138017478554)
XLA Ops:
  0.7 84.5 %stream_attention.1 = bf16[4,40,128]{2,1,0:T(8,128)(2,1)} custom-call(s32[1]{0:T(128)S(6)} %copy.8.vf, bf16[4,40,128]{2,1,0:T(8,128)(2,1)} %q_hbm.1, bf16[256,40,128]{2,1,0:T(8,128)(2,1)} %k_hbm.1, bf16[256,40,128]{2,1,0:T(8,128)(2,1)} %v_hbm.1, bf16[4,40,128]{2,1,0:T(8,128)(2,1)} %nk_hbm.1, bf16[4,40,128]{2,1,0:T(8,128)(2,1)} %nv_hbm.1), custom_call_target="tpu_custom_call" | custom-call | tf_op jit(solution)/shard_map/stream_attention/pallas_call | solution.py:516
  85.2 1.4 %copy.9 = bf16[4,40,128]{2,1,0:T(8,128)(2,1)} copy(bf16[4,40,128]{2,1,0:T(8,128)(2,1)} %stream_attention.1) | data formatting | bytes 81920
